TPU v7x, 32 devices: a whole 2x2x4 slice. The times are simulated.
32 devices in a mesh: tensor: 8 (over z, y), dp: 4 (over x, core).
Axes of the slice: x: 2, y: 2, z: 4, core: 2. Of those that a mesh axis runs over, the one named last changes fastest.
Arguments:
- base_weight: bfloat16 [2, 2, 4096, 14336], P(None, None, 'tensor', 'dp'), may hold values from -0.125 to 0.125
- adapter_left: bfloat16 [2, 2, 4096, 16], P(None, None, 'tensor'), may hold values from -0.059814453 to 0.059814453
- adapter_right: bfloat16 [2, 2, 16, 14336], P(None, None, None, 'dp'), may hold values from -1.5 to 1.5
- magnitude: bfloat16 [2, 2, 14336], P(None, None, 'dp'), may hold values from 16 to 256
Outputs:
- merged_weight: bfloat16 [2, 2, 14336, 4096], P(None, None, 'tensor')
All inputs are finite; a program needn't handle non-finite values.
Results may differ from a plain program's by a relative error of at most 0.0004.
Values may be sent and summed in bfloat16 or wider, within the bound.
A program may use at most 384 MiB of HBM per device.

v0:
```python
import jax
import jax.numpy as jnp
from jax import lax
from jax.sharding import PartitionSpec as P


def regroup(weight_slab):
    experts, projections, row_count, col_count = weight_slab.shape
    tensor_count = lax.axis_size("tensor")
    replica_count = lax.axis_size("dp")
    serve_cols = col_count * replica_count // tensor_count
    quartered = lax.all_to_all(weight_slab, "dp", split_axis=2, concat_axis=3, tiled=True)
    grouped = lax.all_to_all(quartered, "tensor", split_axis=3, concat_axis=2, tiled=True)
    collected = lax.all_gather(grouped, "dp", axis=2, tiled=True)
    pieces_view = collected.reshape(
        experts, projections, replica_count, tensor_count, row_count // replica_count, serve_cols
    )
    return pieces_view.transpose(0, 1, 5, 3, 2, 4).reshape(
        experts, projections, serve_cols, tensor_count * row_count
    )


def shards(base_weight, adapter_left, adapter_right, magnitude):
    tensor_count = lax.axis_size("tensor")
    replica_count = lax.axis_size("dp")
    col_count = base_weight.shape[3]
    serve_cols = col_count * replica_count // tensor_count
    arrived = regroup(base_weight)
    left_full = lax.all_gather(adapter_left, "tensor", axis=2, tiled=True)
    right_all, magnitude_all = (
        lax.all_gather(adapter_right, "dp", axis=3, tiled=True),
        lax.all_gather(magnitude, "dp", axis=2, tiled=True),
    )
    col_start = lax.axis_index("tensor") * serve_cols
    right_cols = lax.dynamic_slice_in_dim(right_all, col_start, serve_cols, 3)
    magnitude_cols = lax.dynamic_slice_in_dim(magnitude_all, col_start, serve_cols, 2)
    merged = arrived.astype(jnp.float32) + jnp.einsum(
        "xyrf,xyir->xyfi", right_cols, left_full, preferred_element_type=jnp.float32
    )
    squares = jnp.sum(merged * merged, axis=3)
    scaling = magnitude_cols.astype(jnp.float32) / jnp.sqrt(squares + 1e-06)
    return (merged * scaling[:, :, :, None]).astype(jnp.bfloat16)


def solution(mesh):
    in_specs = (
        P(None, None, "tensor", "dp"),
        P(None, None, "tensor", None),
        P(None, None, None, "dp"),
        P(None, None, "dp"),
    )
    out_specs = P(None, None, "tensor", None)
    return jax.shard_map(shards, mesh=mesh, in_specs=in_specs, out_specs=out_specs, check_vma=False)
```

profile of v0, /device:TPU:0, one launch (start us, length us, event | category | flops | bytes accessed | tf_op | source)
XLA Modules:
  0.0 1412.7 jit_solution(15380648244559566763)
XLA Ops:
  6.5 0.0 all-gather.3.cloned.1.call-start
  6.5 26.6 %copy.15 = bf16[2,2,512,3584]{3,1,0,2:T(2,128)(2,1)S(1)} copy(bf16[2,2,512,3584]{3,2,1,0:T(8,128)(2,1)} %param.4) | data formatting | bytes 29360128 | tf_op args[0]
  33.2 164.5 %all_to_all.36 = bf16[2,2,512,3584]{3,1,0,2:T(2,128)(2,1)S(1)} all-to-all(bf16[2,2,512,3584]{3,1,0,2:T(2,128)(2,1)S(1)} %copy.15), channel_id=1, replica_groups=mesh['tensor'=8,'dp'=4] {'dp'}, dimensions={2} | all-to-all | bytes 29360128 | tf_op jit(solution)/shard_map/all_to_all | solution.py:12
  197.7 6.8 copy.16
  204.5 18.7 %copy.17 = bf16[2,2,128,4,3584]{2,4,3,1,0:T(8,128)(2,1)} copy(bf16[2,2,128,4,3584]{4,2,3,1,0:T(8,128)(2,1)} %bitcast.15) | data formatting | bytes 29360128 | tf_op jit(solution)/shard_map/all_to_all | solution.py:12
  223.2 24.6 %copy.18 = bf16[2,2,128,14336]{2,1,0,3:T(2,128)(2,1)S(1)} copy(bf16[2,2,128,14336]{2,3,1,0:T(8,128)(2,1)} %bitcast.16) | data formatting | bytes 29360128 | tf_op jit(solution)/shard_map/all_to_all | solution.py:12
  247.7 0.0 copy-start.1
  247.7 0.0 copy-start.2
  247.8 324.4 %all_to_all.37 = bf16[2,2,128,14336]{2,1,0,3:T(2,128)(2,1)S(1)} all-to-all(bf16[2,2,128,14336]{2,1,0,3:T(2,128)(2,1)S(1)} %copy.18), channel_id=1, replica_groups=mesh['tensor'=8,'dp'=4] {'tensor'}, dimensions={3} | all-to-all | bytes 29360128 | tf_op jit(solution)/shard_map/all_to_all | solution.py:13
  572.2 7.8 copy.19
  580.0 18.8 %copy.20 = bf16[2,2,8,128,1792]{4,3,2,1,0:T(8,128)(2,1)} copy(bf16[2,2,8,128,1792]{3,4,2,1,0:T(8,128)(2,1)} %bitcast.17) | data formatting | bytes 29360128 | tf_op jit(solution)/shard_map/all_to_all | solution.py:13
  598.7 0.0 all-gather.3.cloned.1.call-update
  598.8 0.0 all-gather.5.cloned.1.call-start
  598.8 0.7 all-gather.5.cloned.1.call-update
  599.5 0.0 copy-done.1
  599.5 33.3 %all_gather.14 = bf16[2,2,4096,16]{2,3,1,0:T(8,128)(2,1)} all-gather(bf16[2,2,512,16]{2,3,1,0:T(8,128)(2,1)S(1)} %copy-done.1), channel_id=1, replica_groups=mesh['tensor'=8,'dp'=4] {'tensor'}, dimensions={2}, use_global_device_ids=true | all-gather | bytes 589824 | tf_op jit(solution)/shard_map/all_gather | solution.py:29
  632.8 0.0 copy-done.2
  632.8 6.5 all_gather.15
  639.4 302.8 %all-gather.3.cloned.1.call-done = bf16[2,2,4096,1792]{3,2,1,0:T(8,128)(2,1)} async-done(((bf16[2,2,1024,1792]{3,2,1,0:T(8,128)(2,1)}), bf16[2,2,4096,1792]{3,2,1,0:T(8,128)(2,1)}) %all-gather.3.cloned.1.call-update) | async-done | bytes 58720272 | tf_op jit(solution)/shard_map/all_gather | solution.py:14
  942.2 58.1 %convert_bitcast_fusion = f32[2,2,1792,8,4,128]{2,5,3,4,1,0:T(8,128)} fusion(bf16[2,2,4,8,128,1792]{5,4,3,2,1,0:T(8,128)(2,1)} %bitcast.18), kind=kLoop, calls=%fused_computation | loop fusion | flops 29360128 | bytes 176160768 | tf_op jit(solution)/shard_map/convert_element_type | solution.py:37
  1000.2 137.5 %copy.21 = f32[2,2,1792,8,4,128]{5,4,3,2,1,0:T(4,128)} copy(f32[2,2,1792,8,4,128]{2,5,3,4,1,0:T(8,128)} %convert_bitcast_fusion) | data formatting | bytes 234881024 | tf_op jit(solution)/shard_map/convert_element_type | solution.py:37
  1137.8 0.0 copy-start
  1137.8 135.7 %reshape.7 = f32[2,2,1792,4096]{3,2,1,0:T(8,128)} reshape(f32[2,2,1792,8,4,128]{5,4,3,2,1,0:T(4,128)} %copy.21) | data formatting | bytes 234881024 | tf_op jit(solution)/shard_map/convert_element_type | solution.py:37
  1273.5 0.0 all-gather.5.cloned.1.call-done
  1273.5 0.0 copy-done
  1273.5 75.6 %multiply_reduce_fusion = (f32[2,2,1792]{2,1,0:T(2,128)S(1)}, f32[2,2,1792,4096]{3,2,1,0:T(8,128)}) fusion(f32[2,2,1792,4096]{3,2,1,0:T(8,128)} %reshape.7, bf16[2,2,4096,16]{2,3,1,0:T(8,128)(2,1)S(1)} %copy-done, bf16[2,2,16,14336]{3,2,1,0:T(8,128)(2,1)} %all-gather.5.cloned.1.call-done, s32[]{:T(128)S(6)} %select_n.4), kind=kOutput, calls=%fused_computation.2 | convolution fusion | flops 1027597312 | bytes 235663360 | tf_op jit(solution)/shard_map/xyrf,xyir->xyfi/dot_general | solution.py:37
  1349.2 0.7 rsqrt_multiply_fusion
  1349.9 56.0 %multiply_convert_fusion = bf16[2,2,1792,4096]{3,2,1,0:T(8,128)(2,1)} fusion(f32[2,2,1792,4096]{3,2,1,0:T(8,128)} %get-tuple-element.6, f32[2,2,1792]{2,1,0:T(2,128)S(1)} %rsqrt_multiply_fusion), kind=kLoop, calls=%fused_computation.1 | loop fusion | flops 58720256 | bytes 176189440 | tf_op jit(solution)/shard_map/convert_element_type | solution.py:42
Async XLA Ops:
  6.5 935.6 %all-gather.3.cloned.1.call-start = ((), (), s32[]{:S(2)}) async-start(), calls=%async_computation.2 | async-start | bytes 73400320 | tf_op jit(solution)/shard_map/all_gather | solution.py:14
  247.7 351.8 %copy-start.1 = (bf16[2,2,512,16]{2,3,1,0:T(8,128)(2,1)S(1)}, bf16[2,2,512,16]{2,3,1,0:T(8,128)(2,1)}, u32[]{:S(2)}) copy-start(bf16[2,2,512,16]{2,3,1,0:T(8,128)(2,1)} %param.5) | copy-start | bytes 196612
  247.7 385.1 %copy-start.2 = (bf16[2,2,3584]{2,1,0:T(2,128)(2,1)S(1)}, bf16[2,2,3584]{2,1,0:T(2,128)(2,1)}, u32[]{:S(2)}) copy-start(bf16[2,2,3584]{2,1,0:T(2,128)(2,1)} %param.7) | copy-start | bytes 86020
  598.8 674.7 %all-gather.5.cloned.1.call-start = ((), (), s32[]{:S(2)}) async-start(), calls=%async_computation.3 | async-start | bytes 2293760 | tf_op jit(solution)/shard_map/all_gather | solution.py:31
  1137.8 135.8 %copy-start = (bf16[2,2,4096,16]{2,3,1,0:T(8,128)(2,1)S(1)}, bf16[2,2,4096,16]{2,3,1,0:T(8,128)(2,1)}, u32[]{:S(2)}) copy-start(bf16[2,2,4096,16]{2,3,1,0:T(8,128)(2,1)} %all_gather.14) | copy-start | bytes 1572868
Sparse Core Ops, SparseCore 0:
  598.9 343.2 all-gather.2
  943.7 21.0 all-gather.4
where the time goes:
time: 1420 us; the launch traced here: 1410 us
  blocking collectives  529 us (37%)
  local copies, waits for them, and re-layouts  377 us (27%)
  waiting for transfers between devices  304 us (21%)
  other arithmetic  115 us (8%)
  matrix products  75.6 us (5%)
    all_to_all x1, blocking collectives, regroup(): lax.all_to_all(quartered, 'tensor', split_axis=3, concat_axis=2, tiled=True)  324 us
    all_gather x1, waiting for transfers between devices, regroup(): collected = lax.all_gather(grouped, 'dp', axis=2, tiled=True)  303 us
    convert_element_type x2, local copies, waits for them, and re-layouts, shards(): arrived.astype(jnp.float32)  273 us
    all_to_all x1, blocking collectives, regroup(): lax.all_to_all(weight_slab, 'dp', split_axis=2, concat_axis=3, tiled=True)  165 us
    dot_general x1, matrix products, shards(): jnp.einsum('xyrf,xyir->xyfi', right_cols, left_full, preferred_element_ty...  75.6 us
    convert_element_type x1, other arithmetic, shards(): arrived.astype(jnp.float32)  58.1 us
    convert_element_type x1, other arithmetic, shards(): return (merged * scaling[:, :, :, None]).astype(jnp.bfloat16)  56 us
    all_to_all x3, local copies, waits for them, and re-layouts, regroup(): lax.all_to_all(weight_slab, 'dp', split_axis=2, concat_axis=3, tiled=True)  50 us
  transfers between devices with their start and end apart: 2, of which 1 were waited for; matrix products, arithmetic and copies ran while one was open for 23% of the time, Pallas kernels for 0%

commit v1 on v0

v1 whole, which is shorter than its diff:
```python
import functools

import jax
import jax.numpy as jnp
from jax import lax
from jax.experimental import pallas as pl
from jax.experimental.pallas import tpu as pltpu
from jax.sharding import PartitionSpec as P

MESH = pl.DeviceIdType.MESH


def exchange_kernel(sizes, chunks, relayed, s, g, rb, recv, xs, cs, a_send, a_recv, b_send, r_send):
    tensor_count, replica_count = sizes
    group = tensor_count // replica_count
    half_t, half_r = tensor_count // 2, replica_count // 2
    serve = s.shape[3]
    parts = ((0, relayed), (relayed, serve - relayed))
    t, d = lax.axis_index("tensor"), lax.axis_index("dp")
    twin = lax.rem(d + half_r, replica_count)
    mate = d + 1 - 2 * lax.rem(d, 2)
    near = t // half_t == d // half_r
    far = jnp.logical_not(near)
    home = t // group
    is_home, is_twin = home == d, home == twin
    base = (t // half_t) * half_t
    other = half_t - base

    def near_source(i):
        return base + lax.rem(t - base + i, half_t)

    def far_source(i):
        return other + lax.rem(t - base + i, half_t)

    def own(k, j, p):
        return s.at[k, j, :, pl.ds(*parts[p])]

    def slot(ts, k, p):
        return g.at[ts, k, :, pl.ds(*parts[p])]

    def send(src, ts, k, p, sem, tensor, dp):
        return pltpu.make_async_remote_copy(
            src_ref=src, dst_ref=slot(ts, k, p), send_sem=sem, recv_sem=recv.at[ts, k, p],
            device_id={"tensor": tensor, "dp": dp}, device_id_type=MESH,
        )

    def to_twin(src, ts, k, p):
        return send(src, ts, k, p, xs.at[ts, k, p], t, twin)

    def to_mate(src, ts, k, p):
        return send(src, ts, k, p, cs.at[ts, k, p], t, mate)

    def to_relay(k, j):
        return pltpu.make_async_remote_copy(
            src_ref=own(k, j, 0), dst_ref=rb.at[k, j], send_sem=a_send.at[k, j], recv_sem=a_recv.at[k, j],
            device_id={"tensor": t, "dp": twin}, device_id_type=MESH,
        )

    def relay(k, j):
        return send(rb.at[k, j], t, k, 0, r_send.at[k, j], twin * group + j, d)

    def direct(k, j, p):
        return send(own(k, j, p), t, k, p, b_send.at[k, j, p], d * group + j, d)

    def keep(k, p):
        return pltpu.make_async_copy(own(k, lax.rem(t, group), p), slot(t, k, p), recv.at[t, k, p])

    def got(ts, k, p):
        to_mate(slot(ts, k, p), ts, k, p).wait_recv()

    def loop(count, body, first=0):
        lax.fori_loop(first, count, lambda i, c: (body(i), c)[1], 0)

    def each_piece(body):
        loop(chunks, lambda k: loop(group, lambda j: body(k, j)))

    def start_piece(k, j):
        leaves = d * group + j != t

        @pl.when(far)
        def _():
            to_relay(k, j).start()
            direct(k, j, 1).start()

        @pl.when(jnp.logical_and(near, leaves))
        def _():
            direct(k, j, 0).start()
            direct(k, j, 1).start()

        @pl.when(jnp.logical_not(leaves))
        def _():
            for p in range(2):
                src = own(k, j, p)
                to_twin(src, t, k, p).start()
                to_mate(src, t, k, p).start()
                keep(k, p).start()

    each_piece(start_piece)

    def pass_on(ts, k, p):
        got(ts, k, p)
        to_twin(slot(ts, k, p), ts, k, p).start()
        to_mate(slot(ts, k, p), ts, k, p).start()

    def hand_over(ts, k, p):
        got(ts, k, p)
        to_mate(slot(ts, k, p), ts, k, p).start()

    def relay_step(k):
        @pl.when(near)
        def _():
            def one(j):
                to_relay(k, j).wait_recv()
                relay(k, j).start()

            loop(group, one)

    def arrivals(k):
        @pl.when(is_home)
        def _():
            def one(i):
                pass_on(near_source(i), k, 0)
                pass_on(near_source(i), k, 1)

            loop(half_t, one, 1)
            loop(half_t, lambda i: pass_on(far_source(i), k, 1))

        @pl.when(is_twin)
        def _():
            loop(half_t, lambda i: pass_on(far_source(i), k, 0))

    def second_hand(k):
        @pl.when(is_home)
        def _():
            loop(half_t, lambda i: hand_over(far_source(i), k, 0))

        @pl.when(is_twin)
        def _():
            def one(i):
                hand_over(near_source(i), k, 0)
                hand_over(near_source(i), k, 1)

            loop(half_t, one)
            loop(half_t, lambda i: hand_over(far_source(i), k, 1))

    relay_step(0)

    def step(k):
        @pl.when(k + 1 < chunks)
        def _():
            relay_step(k + 1)

        arrivals(k)

        @pl.when(k > 0)
        def _():
            second_hand(k - 1)

    loop(chunks, step)
    second_hand(chunks - 1)

    serving = jnp.logical_or(is_home, is_twin)

    @pl.when(jnp.logical_not(serving))
    def _():
        def one(k, ts):
            got(ts, k, 0)
            got(ts, k, 1)

        loop(chunks, lambda k: loop(tensor_count, lambda ts: one(k, ts)))

    @pl.when(is_home)
    def _():
        def one(k):
            keep(k, 0).wait()
            keep(k, 1).wait()

        loop(chunks, one)

    def finish_piece(k, j):
        leaves = d * group + j != t

        @pl.when(far)
        def _():
            to_relay(k, j).wait_send()
            direct(k, j, 1).wait_send()

        @pl.when(near)
        def _():
            relay(k, j).wait_send()

        @pl.when(jnp.logical_and(near, leaves))
        def _():
            direct(k, j, 0).wait_send()
            direct(k, j, 1).wait_send()

    each_piece(finish_piece)

    @pl.when(serving)
    def _():
        def one(k, ts):
            to_mate(slot(ts, k, 0), ts, k, 0).wait_send()
            to_mate(slot(ts, k, 1), ts, k, 1).wait_send()

        loop(chunks, lambda k: loop(tensor_count, lambda ts: one(k, ts)))

    @pl.when(is_home)
    def _():
        def one(k, i):
            to_twin(slot(near_source(i), k, 0), near_source(i), k, 0).wait_send()
            to_twin(slot(near_source(i), k, 1), near_source(i), k, 1).wait_send()
            to_twin(slot(far_source(i), k, 1), far_source(i), k, 1).wait_send()

        loop(chunks, lambda k: loop(half_t, lambda i: one(k, i)))

    @pl.when(is_twin)
    def _():
        def one(k, i):
            to_twin(slot(far_source(i), k, 0), far_source(i), k, 0).wait_send()

        loop(chunks, lambda k: loop(half_t, lambda i: one(k, i)))


def exchange(s, tensor_count, replica_count, relayed):
    chunks, group, each, serve, rows = s.shape
    dma = pltpu.SemaphoreType.DMA
    g, _ = pl.pallas_call(
        functools.partial(exchange_kernel, (tensor_count, replica_count), chunks, relayed),
        out_shape=(
            jax.ShapeDtypeStruct((tensor_count, chunks, each, serve, rows), s.dtype),
            jax.ShapeDtypeStruct((chunks, group, each, relayed, rows), s.dtype),
        ),
        in_specs=[pl.BlockSpec(memory_space=pl.ANY)],
        out_specs=[pl.BlockSpec(memory_space=pl.ANY)] * 2,
        scratch_shapes=[dma((tensor_count, chunks, 2))] * 3
        + [dma((chunks, group))] * 2
        + [dma((chunks, group, 2)), dma((chunks, group))],
        compiler_params=pltpu.CompilerParams(has_side_effects=True),
    )(s)
    return g


def flip_kernel(w, o):
    o[0] = w[0].T


def flip(w):
    stacks, rows, cols = w.shape
    if rows % 128:
        return w.swapaxes(1, 2)
    wide = next(n for n in (512, 256, 128, cols) if cols % n == 0)
    return pl.pallas_call(
        flip_kernel,
        grid=(stacks, cols // wide),
        in_specs=[pl.BlockSpec((1, rows, wide), lambda e, c: (e, 0, c))],
        out_specs=pl.BlockSpec((1, wide, rows), lambda e, c: (e, c, 0)),
        out_shape=jax.ShapeDtypeStruct((stacks, cols, rows), w.dtype),
    )(w)


def merge_kernel(count, rows, g, left, right, magnitude, o, merged):
    squares = None
    for n in range(count):
        at = slice(n * rows, (n + 1) * rows)
        piece = g[n, 0].astype(jnp.float32) + jnp.dot(
            right[0], left[0, :, at], preferred_element_type=jnp.float32
        )
        merged[:, at] = piece
        total = jnp.sum(piece * piece, axis=1, keepdims=True)
        squares = total if squares is None else squares + total
    scaling = magnitude[0].astype(jnp.float32) / jnp.sqrt(squares + 1e-06)
    for n in range(count):
        at = slice(n * rows, (n + 1) * rows)
        o[0, :, at] = (merged[:, at] * scaling).astype(o.dtype)


def merge(g, left, right, magnitude):
    count, stacks, serve, rows = g.shape
    rank = right.shape[2]
    if rows % 128:
        joined = g.transpose(1, 2, 0, 3).reshape(stacks, serve, count * rows)
        merged = joined.astype(jnp.float32) + jnp.einsum(
            "xfr,xri->xfi", right, left, preferred_element_type=jnp.float32
        )
        squares = jnp.sum(merged * merged, axis=2, keepdims=True)
        scaling = magnitude.astype(jnp.float32) / jnp.sqrt(squares + 1e-06)
        return (merged * scaling).astype(g.dtype)
    tall = next(n for n in (256, 128, 64, 32, 16, serve) if serve % n == 0)
    return pl.pallas_call(
        functools.partial(merge_kernel, count, rows),
        grid=(stacks, serve // tall),
        in_specs=[
            pl.BlockSpec((count, 1, tall, rows), lambda e, f: (0, e, f, 0)),
            pl.BlockSpec((1, rank, count * rows), lambda e, f: (e, 0, 0)),
            pl.BlockSpec((1, tall, rank), lambda e, f: (e, f, 0)),
            pl.BlockSpec((1, tall, 1), lambda e, f: (e, f, 0)),
        ],
        out_specs=pl.BlockSpec((1, tall, count * rows), lambda e, f: (e, f, 0)),
        out_shape=jax.ShapeDtypeStruct((stacks, serve, count * rows), g.dtype),
        scratch_shapes=[pltpu.VMEM((tall, count * rows), jnp.float32)],
    )(g, left, right, magnitude)


def shards(base_weight, adapter_left, adapter_right, magnitude):
    tensor_count = lax.axis_size("tensor")
    replica_count = lax.axis_size("dp")
    experts, projections, rows, cols = base_weight.shape
    rank = adapter_left.shape[3]
    stacks = experts * projections
    group = tensor_count // replica_count
    serve = cols // group
    chunks = stacks if tensor_count <= 16 else 1
    relayed = (2 * (serve // 16) + 1) // 3 * 16

    s = flip(base_weight.reshape(stacks, rows, cols))
    if chunks == 1:
        s = s.reshape(1, stacks, group, serve, rows).swapaxes(1, 2)
    else:
        s = s.reshape(chunks, group, 1, serve, rows)
    g = exchange(s, tensor_count, replica_count, relayed).reshape(tensor_count, stacks, serve, rows)

    left = lax.all_gather(adapter_left.swapaxes(2, 3), "tensor", axis=3, tiled=True)
    right_all = lax.all_gather(adapter_right, "dp", axis=3, tiled=True)
    magnitude_all = lax.all_gather(magnitude, "dp", axis=2, tiled=True)
    start = lax.axis_index("tensor") * serve
    right = lax.dynamic_slice_in_dim(right_all, start, serve, 3).swapaxes(2, 3)
    strength = lax.dynamic_slice_in_dim(magnitude_all, start, serve, 2)
    out = merge(
        g,
        left.reshape(stacks, rank, -1),
        right.reshape(stacks, serve, rank),
        strength.reshape(stacks, serve, 1),
    )
    return out.reshape(experts, projections, serve, -1)


def solution(mesh):
    in_specs = (
        P(None, None, "tensor", "dp"),
        P(None, None, "tensor", None),
        P(None, None, None, "dp"),
        P(None, None, "dp"),
    )
    out_specs = P(None, None, "tensor", None)
    return jax.shard_map(shards, mesh=mesh, in_specs=in_specs, out_specs=out_specs, check_vma=False)
```

time: 1420 us -> 662 us (0.47)
  Pallas kernels: 0 us -> 576 us
  blocking collectives: 529 us -> 63 us
  local copies, waits for them, and re-layouts: 377 us -> 7.72 us
  waiting for transfers between devices: 304 us -> 0.71 us
  other arithmetic: 115 us -> 0 us
  matrix products: 75.6 us -> 0 us
    pallas_call x0 -> x3, Pallas kernels: none -> 576 us  [the longest x1 495 us: exchange(): pl.pallas_call(functools.partial(exchange_kernel, (tensor_count, replica_...]
    all_to_all x2 -> x0, blocking collectives: 489 us -> none  [the longest x1 324 us: regroup(): lax.all_to_all(quartered, 'tensor', split_axis=3, concat_axis=2, tiled=True)]
    all_gather x2 -> x1, waiting for transfers between devices: 303 us -> 0.01 us  [shards(): right_all = lax.all_gather(adapter_right, 'dp', axis=3, tiled=True)]
    convert_element_type x2 -> x0, local copies, waits for them, and re-layouts: 273 us -> none  [shards(): arrived.astype(jnp.float32)]
    convert_element_type x2 -> x0, other arithmetic: 114 us -> none  [the longest x1 58.1 us: shards(): arrived.astype(jnp.float32)]
    all_to_all x5 -> x0, local copies, waits for them, and re-layouts: 76.6 us -> none  [the longest x3 50 us: regroup(): lax.all_to_all(weight_slab, 'dp', split_axis=2, concat_axis=3, tiled=True)]
    dot_general x1 -> x0, matrix products: 75.6 us -> none  [shards(): jnp.einsum('xyrf,xyir->xyfi', right_cols, left_full, preferred_element_ty...]
    unnamed x7 -> x2, local copies, waits for them, and re-layouts: 26.6 us -> 0.01 us
  transfers between devices with their start and end apart: 2 -> 1, of which waited for: 1 -> 0; matrix products, arithmetic and copies ran while one was open for 23% -> 1% of each run, Pallas kernels for 0% -> 78%
where the time goes in v1:
time: 662 us; the launch traced here: 661 us
  Pallas kernels  576 us (87%)
  blocking collectives  63 us (10%)
  between operations  13.4 us (2%)
  local copies, waits for them, and re-layouts  7.72 us (1%)
    pallas_call x1, Pallas kernels, exchange(): pl.pallas_call(functools.partial(exchange_kernel, (tensor_count, replica_...  495 us
    pallas_call x1, Pallas kernels, merge(): pl.pallas_call(functools.partial(merge_kernel, count, rows), grid=(stacks...  58.5 us
    all_gather x1, blocking collectives, shards(): lax.all_gather(adapter_left.swapaxes(2, 3), 'tensor', axis=3, tiled=True)  56.4 us
    pallas_call x1, Pallas kernels, flip(): pl.pallas_call(flip_kernel, grid=(stacks, cols // wide), in_specs=[pl.Blo...  21.9 us
  transfers between devices with their start and end apart: 1, of which 0 were waited for; matrix products, arithmetic and copies ran while one was open for 1% of the time, Pallas kernels for 78%

profile of v1, /device:TPU:0, one launch (start us, length us, event | category | flops | bytes accessed | tf_op | source)
XLA Modules:
  0.0 660.6 jit_solution(13612785062895768270)
XLA Ops:
  6.5 0.0 all-gather.2.cloned.1.call-start
  6.5 0.7 all-gather.2.cloned.1.call-update
  7.3 6.6 %all_gather.11 = bf16[2,2,14336]{2,1,0:T(2,128)(2,1)S(1)} all-gather(bf16[2,2,3584]{2,1,0:T(2,128)(2,1)} %param.7), channel_id=1, replica_groups=mesh['tensor'=8,'dp'=4] {'dp'}, dimensions={2}, use_global_device_ids=true | all-gather | bytes 143360 | tf_op jit(solution)/shard_map/all_gather | solution.py:324
  13.9 5.1 reshape.28.magnitude
  19.0 21.9 %shard_map.46 = bf16[4,3584,512]{2,1,0:T(8,128)(2,1)} custom-call(bf16[4,512,3584]{2,1,0:T(8,128)(2,1)} %bitcast.11), custom_call_target="tpu_custom_call" | custom-call | tf_op jit(solution)/shard_map/pallas_call | solution.py:252
  41.0 0.0 copy-start
  41.0 495.3 %shard_map.47 = (bf16[8,4,1,1792,512]{4,3,2,1,0:T(8,128)(2,1)}, bf16[4,2,1,1200,512]{4,3,2,1,0:T(8,128)(2,1)}) custom-call(bf16[4,2,1,1792,512]{4,3,2,1,0:T(8,128)(2,1)} %bitcast.9), custom_call_target="tpu_custom_call" | custom-call | tf_op jit(solution)/shard_map/pallas_call | solution.py:227
  536.3 0.0 copy-done
  536.3 56.4 %all_gather.9 = bf16[2,2,16,4096]{3,2,1,0:T(8,128)(2,1)} all-gather(bf16[2,2,16,512]{3,2,1,0:T(8,128)(2,1)S(1)} %bitcast.14), channel_id=1, replica_groups=mesh['tensor'=8,'dp'=4] {'tensor'}, dimensions={3}, use_global_device_ids=true | all-gather | bytes 589824 | tf_op jit(solution)/shard_map/all_gather | solution.py:322
  592.7 0.0 all-gather.2.cloned.1.call-done
  592.7 1.0 dynamic-slice_bitcast_fusion
  593.6 1.6 copy.6
  595.2 58.5 %shard_map.48 = bf16[4,1792,4096]{2,1,0:T(8,128)(2,1)} custom-call(bf16[8,4,1792,512]{3,2,1,0:T(8,128)(2,1)} %bitcast.10, bf16[4,16,4096]{2,1,0:T(8,128)(2,1)} %bitcast.13, bf16[4,1792,16]{2,1,0:T(8,128)(2,1)} %bitcast.12, bf16[4,1792,1]{2,1,0:T(8,128)(2,1)} %reshape.28.magnitude), custom_call_target="tpu_custom_call" | custom-call | tf_op jit(solution)/shard_map/pallas_call | solution.py:289
  (1 shorter events, 0.0 us)
Async XLA Ops:
  6.5 586.1 %all-gather.2.cloned.1.call-start = ((), (), s32[]{:S(2)}) async-start(), calls=%async_computation | async-start | bytes 2293760 | tf_op jit(solution)/shard_map/all_gather | solution.py:323
  41.0 495.3 %copy-start = (bf16[2,2,512,16]{2,3,1,0:T(8,128)(2,1)S(1)}, bf16[2,2,512,16]{2,3,1,0:T(8,128)(2,1)}, u32[]{:S(2)}) copy-start(bf16[2,2,512,16]{2,3,1,0:T(8,128)(2,1)} %param.5) | copy-start | bytes 196612
Sparse Core Ops, SparseCore 0:
  8.9 23.8 all-gather.1
